TPU v7x, 32 devices: a whole 2x2x4 slice. The times are simulated.
32 devices in a mesh: path: 8 (over y, x, core), mod: 4 (over z).
Axes of the slice: x: 2, y: 2, z: 4, core: 2. Of those that a mesh axis runs over, the one named last changes fastest.
Arguments:
- activations: bfloat16 [8, 512, 4096], P('path', 'mod'), may hold values from -6 to 6
- cotangent: bfloat16 [8, 512, 4096], P('path', 'mod'), may hold values from -6 to 6
- first_weight: bfloat16 [8, 4096, 4096], P('path', None, 'mod'), may hold values from -6 to 6
- second_weight: bfloat16 [8, 4096, 4096], P('path', None, 'mod'), may hold values from -6 to 6
- first_master: float32 [4, 4096, 4096], P(None, ('path', 'mod')), may hold values from -6 to 6
- second_master: float32 [4, 4096, 4096], P(None, ('path', 'mod')), may hold values from -6 to 6
- first_moment: float32 [4, 4096, 4096], P(None, ('path', 'mod')), may hold values from -3 to 3
- second_moment: float32 [4, 4096, 4096], P(None, ('path', 'mod')), may hold values from -3 to 3
- routing: int32 [8, 2], replicated, may hold values from 0 to 3, as said below
Outputs:
- first_result: bfloat16 [8, 4096, 4096], P('path', None, 'mod')
- second_result: bfloat16 [8, 4096, 4096], P('path', None, 'mod')
Inputs may be any that keep to these rules, and one draw needn't show every extreme that they name: `routing`: for each of the two levels, every one of the 4 modules is taken by at least one path.
All inputs are finite; a program needn't handle non-finite values.
Results may differ from a plain program's by a relative error of at most 0.0045.
Values may be sent and summed in bfloat16 or wider, within the bound.
A program may use at most 192 MiB of HBM per device.

v0:
```python
import jax
import jax.numpy as jnp
from jax import lax
from jax.sharding import PartitionSpec as P

inner_rate = 1.0
outer_rate = 0.7
momentum_decay = 0.9


def to_owners(stacked, onehot):
    level_count = stacked.shape[0]
    columns = stacked.shape[2]
    path_count = onehot.shape[1]
    groups = lax.axis_size("mod")
    arrived = lax.all_to_all(stacked, ("path", "mod"), split_axis=1, concat_axis=2, tiled=True)
    owned_rows = arrived.shape[1]
    arrived = arrived.reshape(level_count, owned_rows, path_count, groups, columns)
    summed = jnp.einsum("lrpkc,lpm->lmrkc", arrived, onehot, preferred_element_type=jnp.float32)
    return summed.reshape(level_count, onehot.shape[2], owned_rows, groups * columns)


def outer_step(summed, onehot, master, moment):
    path_total = jnp.sum(onehot.astype(jnp.float32), axis=1)[:, :, None, None]
    outer = master - summed / path_total
    moment_new = momentum_decay * moment + outer
    return (master - outer_rate * (outer + momentum_decay * moment_new)).astype(jnp.bfloat16)


def to_paths(renewed, onehot):
    level_count, module_count, owned_rows, model_width = renewed.shape
    groups = lax.axis_size("mod")
    path_count = onehot.shape[1]
    columns = model_width // groups
    split = renewed.reshape(level_count, module_count, owned_rows, groups, columns)
    chosen = jnp.einsum(
        "lmrkc,lpm->lrpkc", split, onehot, preferred_element_type=jnp.float32
    ).astype(jnp.bfloat16)
    outgoing = chosen.reshape(level_count, owned_rows, path_count * groups * columns)
    return lax.all_to_all(outgoing, ("path", "mod"), split_axis=2, concat_axis=1, tiled=True)


def body(
    activations,
    cotangent,
    first_weight,
    second_weight,
    first_master,
    second_master,
    first_moment,
    second_moment,
    routing,
):
    inputs_full, upstream = (
        lax.all_gather(activations, "mod", axis=1, tiled=True),
        lax.all_gather(cotangent, "mod", axis=1, tiled=True),
    )
    inputs_full = inputs_full[0]
    upstream = upstream[0]
    weight_in = first_weight[0]
    weight_out = second_weight[0]
    scale = inputs_full.shape[1] ** (-0.5)
    pre = jnp.dot(inputs_full, weight_in, preferred_element_type=jnp.float32) * scale
    hidden = jax.nn.silu(pre).astype(jnp.bfloat16)
    grad_hidden = jnp.dot(upstream, weight_out, preferred_element_type=jnp.float32) * scale
    grad_out = (
        lax.dot_general(
            upstream, hidden, (((0,), (0,)), ((), ())), preferred_element_type=jnp.float32
        )
        * scale
    )
    trained_out = (weight_out.astype(jnp.float32) - inner_rate * grad_out).astype(jnp.bfloat16)
    sigma = jax.nn.sigmoid(pre)
    grad_pre = (grad_hidden * sigma * (1.0 + pre * (1.0 - sigma))).astype(jnp.bfloat16)
    grad_in = (
        lax.dot_general(
            inputs_full, grad_pre, (((0,), (0,)), ((), ())), preferred_element_type=jnp.float32
        )
        * scale
    )
    trained_in = (weight_in.astype(jnp.float32) - inner_rate * grad_in).astype(jnp.bfloat16)
    module_count = first_master.shape[0]
    module_ids = jnp.arange(module_count)
    onehot = (jnp.transpose(routing)[:, :, None] == module_ids[None, None, :]).astype(jnp.bfloat16)
    summed = to_owners(jnp.stack((trained_in, trained_out)), onehot)
    renewed = outer_step(
        summed,
        onehot,
        jnp.stack((first_master, second_master)),
        jnp.stack((first_moment, second_moment)),
    )
    returned = to_paths(renewed, onehot)
    first_back = returned[0]
    second_back = returned[1]
    return (first_back[None], second_back[None])


def solution(mesh):
    return jax.shard_map(
        body,
        mesh=mesh,
        in_specs=(
            P("path", "mod", None),
            P("path", "mod", None),
            P("path", None, "mod"),
            P("path", None, "mod"),
            P(None, ("path", "mod"), None),
            P(None, ("path", "mod"), None),
            P(None, ("path", "mod"), None),
            P(None, ("path", "mod"), None),
            P(),
        ),
        out_specs=(P("path", None, "mod"), P("path", None, "mod")),
        check_vma=False,
    )
```

profile of v0, /device:TPU:1, one launch (start us, length us, event | category | flops | bytes accessed | tf_op | source)
XLA Modules:
  0.0 1153.4 jit_solution(4697887328991194632)
XLA Ops:
  7.2 0.7 all-gather.5.cloned.1.call-update
  7.9 0.0 all-gather.3.cloned.1.call-start
  7.9 0.7 all-gather.3.cloned.1.call-update
  8.6 12.0 %copy.45 = bf16[1,4096,1024]{1,2,0:T(8,128)(2,1)} copy(bf16[1,4096,1024]{2,1,0:T(8,128)(2,1)} %param.11) | data formatting | bytes 16777216 | tf_op args[2]
  20.6 11.9 %copy.46 = bf16[1,4096,1024]{1,2,0:T(8,128)(2,1)} copy(bf16[1,4096,1024]{2,1,0:T(8,128)(2,1)} %param.12) | data formatting | bytes 16777216 | tf_op args[3]
  32.6 59.7 %all-gather.5.cloned.1.call-done = bf16[1,512,4096]{2,1,0:T(8,128)(2,1)} async-done(((bf16[1,128,4096]{2,1,0:T(8,128)(2,1)}), bf16[1,512,4096]{2,1,0:T(8,128)(2,1)}) %all-gather.5.cloned.1.call-update) | async-done | bytes 4194320 | tf_op jit(solution)/shard_map/all_gather | solution.py:55
  92.2 8.1 fusion.14
  100.4 72.7 %all-gather.3.cloned.1.call-done = bf16[1,512,4096]{2,1,0:T(8,128)(2,1)} async-done(((bf16[1,128,4096]{2,1,0:T(8,128)(2,1)}), bf16[1,512,4096]{2,1,0:T(8,128)(2,1)}) %all-gather.3.cloned.1.call-update) | async-done | bytes 4194320 | tf_op jit(solution)/shard_map/all_gather | solution.py:56
  173.1 18.0 %fusion.18 = bf16[1,4096,1024]{1,2,0:T(8,128)(2,1)} fusion(bf16[1,4096,1024]{1,2,0:T(8,128)(2,1)} %copy.45, bf16[1,512,4096]{2,1,0:T(8,128)(2,1)} %all-gather.5.cloned.1.call-done, f32[512,1024]{1,0:T(8,128)S(1)} %fusion.14, bf16[1,4096,1024]{2,1,0:T(8,128)(2,1)} %param.12, bf16[1,512,4096]{2,1,0:T(8,128)(2,1)} %all-gather.3.cloned.1.call-done), kind=kOutput, calls=%fused_computation.21 | convolution fusion | flops 8612478976 | bytes 35651584 | tf_op jit(solution)/shard_map/dot_general | solution.py:76
  191.1 11.1 fusion.19
  202.1 10.5 pad_maximum_fusion.1
  212.6 41.5 %copy.47 = bf16[2,4096,1024]{2,0,1:T(2,128)(2,1)} copy(bf16[2,4096,1024]{1,2,0:T(8,128)(2,1)} %pad_maximum_fusion.1) | data formatting | bytes 33554432 | tf_op jit(solution)/shard_map/stack | solution.py:85
  254.1 4.2 all-to-all-start
  258.4 8.9 copy.41
  267.3 10.4 copy.43
  277.7 8.9 copy.42
  286.6 10.3 copy.44
  296.9 8.9 copy.50
  305.8 10.4 copy.52
  316.2 8.9 copy.51
  325.0 10.3 copy.53
  335.3 0.1 convert_reduce_fusion
  335.4 280.1 %all-to-all-done = bf16[2,4096,1024]{2,0,1:T(2,128)(2,1)} async-done(((bf16[2,4096,1024]{2,0,1:T(2,128)(2,1)}), bf16[2,4096,1024]{2,0,1:T(2,128)(2,1)}, u32[]{:S(2)}, u32[]{:S(2)}) %all-to-all-start) | async-done | bytes 16777248 | tf_op jit(solution)/shard_map/all_to_all | solution.py:16
  615.5 16.4 %copy.48 = bf16[2,4096,1024]{2,1,0:T(8,128)(2,1)} copy(bf16[2,4096,1024]{2,0,1:T(2,128)(2,1)} %all-to-all-done) | data formatting | bytes 33554432 | tf_op jit(solution)/shard_map/all_to_all | solution.py:16
  632.0 40.2 %convert_bitcast_fusion = bf16[2,128,8,4,1024]{4,2,3,1,0:T(8,128)(2,1)} fusion(f32[1,4,128,4,1024]{4,1,3,2,0:T(4,128)} %copy.53, f32[1,4,128,4,1024]{4,1,3,2,0:T(4,128)} %copy.52, bf16[2,128,8,4,1024]{4,1,3,2,0:T(8,128)(2,1)} %bitcast.86, f32[1,4,128,4,1024]{4,1,3,2,0:T(4,128)} %copy.44, f32[1,4,128,4,1024]{4,1,3,2,0:T(4,128)} %copy.43, ...), kind=kOutput, calls=%fused_computation.15 | convolution fusion | flops 188743808 | bytes 67108960 | tf_op jit(solution)/shard_map/lmrkc,lpm->lrpkc/dot_general | solution.py:36
  672.2 23.0 %copy.54 = bf16[2,128,8,4,1024]{1,4,3,2,0:T(8,128)(2,1)} copy(bf16[2,128,8,4,1024]{4,2,3,1,0:T(8,128)(2,1)} %convert_bitcast_fusion) | data formatting | bytes 33554432 | tf_op jit(solution)/shard_map/convert_element_type | solution.py:38
  695.2 30.0 %copy.55 = bf16[2,128,32768]{1,0,2:T(2,128)(2,1)S(1)} copy(bf16[2,128,32768]{1,2,0:T(8,128)(2,1)} %bitcast.81) | data formatting | bytes 33554432 | tf_op jit(solution)/shard_map/reshape | solution.py:39
  725.2 381.5 %all_to_all.30 = bf16[2,128,32768]{1,0,2:T(2,128)(2,1)} all-to-all(bf16[2,128,32768]{1,0,2:T(2,128)(2,1)S(1)} %copy.55), channel_id=1, replica_groups=mesh['path'=8,'mod'=4] {'path','mod'}, dimensions={2} | all-to-all | bytes 33554432 | tf_op jit(solution)/shard_map/all_to_all | solution.py:40
  1106.8 9.6 copy.56
  1116.4 6.3 fusion.51
  1122.7 11.9 %copy.57 = bf16[1,32,128,1024]{3,2,1,0:T(8,128)(2,1)} copy(bf16[1,32,128,1024]{2,3,1,0:T(8,128)(2,1)} %get-tuple-element.3) | data formatting | bytes 16777216 | tf_op jit(solution)/shard_map/slice | solution.py:93
  1134.6 11.9 %copy.58 = bf16[1,32,128,1024]{3,2,1,0:T(8,128)(2,1)} copy(bf16[1,32,128,1024]{2,3,1,0:T(8,128)(2,1)} %get-tuple-element.2) | data formatting | bytes 16777216 | tf_op jit(solution)/shard_map/slice | solution.py:94
  (5 shorter events, 0.0 us)
Async XLA Ops:
  7.2 85.1 %all-gather.5.cloned.1.call-start = ((), (), s32[]{:S(2)}) async-start(), calls=%async_computation.3 | async-start | bytes 5242880 | tf_op jit(solution)/shard_map/all_gather | solution.py:55
  7.9 165.2 %all-gather.3.cloned.1.call-start = ((), (), s32[]{:S(2)}) async-start(), calls=%async_computation.2 | async-start | bytes 5242880 | tf_op jit(solution)/shard_map/all_gather | solution.py:56
  191.1 11.1 copy-start
  254.1 361.4 %all-to-all-start = ((bf16[2,4096,1024]{2,0,1:T(2,128)(2,1)}), bf16[2,4096,1024]{2,0,1:T(2,128)(2,1)}, u32[]{:S(2)}, u32[]{:S(2)}) async-start(bf16[2,4096,1024]{2,0,1:T(2,128)(2,1)} %copy.47), calls=%async_computation | async-start | bytes 33554432 | tf_op jit(solution)/shard_map/all_to_all | solution.py:16
  325.0 10.3 copy-start.1
Sparse Core Ops, SparseCore 0:
  9.5 82.6 all-gather.4
  93.8 79.2 all-gather.2
where the time goes:
time: 1160 us; the launch traced here: 1150 us
  waiting for transfers between devices  414 us (36%)
  blocking collectives  382 us (33%)
  local copies, waits for them, and re-layouts  252 us (22%)
  matrix products  77.4 us (7%)
  between operations  14.1 us (1%)
    all_to_all x1, blocking collectives, to_paths(): lax.all_to_all(outgoing, ('path', 'mod'), split_axis=2, concat_axis=1, ti...  382 us
    all_to_all x1, waiting for transfers between devices, to_owners(): lax.all_to_all(stacked, ('path', 'mod'), split_axis=1, concat_axis=2, til...  280 us
    all_gather x1, waiting for transfers between devices, body(): lax.all_gather(cotangent, 'mod', axis=1, tiled=True)  72.7 us
    all_gather x1, waiting for transfers between devices, body(): lax.all_gather(activations, 'mod', axis=1, tiled=True)  59.7 us
    unnamed x10, local copies, waits for them, and re-layouts  59.5 us
    another operation x1, local copies, waits for them, and re-layouts, body(): summed = to_owners(jnp.stack((trained_in, trained_out)), onehot)  41.5 us
    dot_general x1, matrix products, to_paths(): jnp.einsum('lmrkc,lpm->lrpkc', split, onehot, preferred_element_type=jnp....  40.2 us
    reshape x1, local copies, waits for them, and re-layouts, to_paths(): chosen.reshape(level_count, owned_rows, path_count * groups * columns)  30 us
  transfers between devices with their start and end apart: 3, of which 3 were waited for; matrix products, arithmetic and copies ran while one was open for 9% of the time, Pallas kernels for 0%

commit v1 on v0

--- a/solution.py
+++ b/solution.py
@@ -37,7 +37,15 @@
         "lmrkc,lpm->lrpkc", split, onehot, preferred_element_type=jnp.float32
     ).astype(jnp.bfloat16)
     outgoing = chosen.reshape(level_count, owned_rows, path_count * groups * columns)
-    return lax.all_to_all(outgoing, ("path", "mod"), split_axis=2, concat_axis=1, tiled=True)
+    return jnp.concatenate(
+        lax.all_to_all(
+            jnp.stack(jnp.split(outgoing, lax.axis_size(("path", "mod")), axis=2)),
+            ("path", "mod"),
+            0,
+            0,
+        ),
+        axis=1,
+    )
 
 
 def body(

time: 1160 us -> 1140 us (0.983)
  local copies, waits for them, and re-layouts: 252 us -> 232 us
    reshape x1 -> x0, local copies, waits for them, and re-layouts: 30 us -> none  [to_paths(): chosen.reshape(level_count, owned_rows, path_count * groups * columns)]
    unnamed x10 -> x43, local copies, waits for them, and re-layouts: 59.5 us -> 79.5 us
  transfers between devices with their start and end apart: 3 -> 3, of which waited for: 3 -> 3; matrix products, arithmetic and copies ran while one was open for 9% -> 10% of each run, Pallas kernels for 0% -> 0%
where the time goes in v1:
time: 1140 us; the launch traced here: 1130 us
  waiting for transfers between devices  414 us (36%)
  blocking collectives  381 us (33%)
  local copies, waits for them, and re-layouts  232 us (20%)
  matrix products  77.4 us (7%)
  between operations  14.2 us (1%)
    all_to_all x1, blocking collectives, to_paths(): lax.all_to_all(jnp.stack(jnp.split(outgoing, lax.axis_size(('path', 'mod'...  381 us
    all_to_all x1, waiting for transfers between devices, to_owners(): lax.all_to_all(stacked, ('path', 'mod'), split_axis=1, concat_axis=2, til...  280 us
    unnamed x43, local copies, waits for them, and re-layouts  79.5 us
    all_gather x1, waiting for transfers between devices, body(): lax.all_gather(cotangent, 'mod', axis=1, tiled=True)  72.7 us
    all_gather x1, waiting for transfers between devices, body(): lax.all_gather(activations, 'mod', axis=1, tiled=True)  59.7 us
    another operation x1, local copies, waits for them, and re-layouts, body(): summed = to_owners(jnp.stack((trained_in, trained_out)), onehot)  41.6 us
    dot_general x1, matrix products, to_paths(): jnp.einsum('lmrkc,lpm->lrpkc', split, onehot, preferred_element_type=jnp....  40.2 us
    convert_element_type x1, local copies, waits for them, and re-layouts, to_paths(): chosen = jnp.einsum('lmrkc,lpm->lrpkc', split, onehot, preferred_element_...  22.9 us
  transfers between devices with their start and end apart: 3, of which 3 were waited for; matrix products, arithmetic and copies ran while one was open for 10% of the time, Pallas kernels for 0%

profile of v1, /device:TPU:1, one launch (start us, length us, event | category | flops | bytes accessed | tf_op | source)
XLA Modules:
  0.0 1133.8 jit_solution(13769484524264929159)
XLA Ops:
  8.6 12.0 %copy.76 = bf16[1,4096,1024]{1,2,0:T(8,128)(2,1)} copy(bf16[1,4096,1024]{2,1,0:T(8,128)(2,1)} %param.11) | data formatting | bytes 16777216 | tf_op args[2]
  20.6 11.9 %copy.77 = bf16[1,4096,1024]{1,2,0:T(8,128)(2,1)} copy(bf16[1,4096,1024]{2,1,0:T(8,128)(2,1)} %param.12) | data formatting | bytes 16777216 | tf_op args[3]
  32.6 59.7 %all-gather.5.cloned.1.call-done = bf16[1,512,4096]{2,1,0:T(8,128)(2,1)} async-done(((bf16[1,128,4096]{2,1,0:T(8,128)(2,1)}), bf16[1,512,4096]{2,1,0:T(8,128)(2,1)}) %all-gather.5.cloned.1.call-update) | async-done | bytes 4194320 | tf_op jit(solution)/shard_map/all_gather | solution.py:63
  92.2 8.1 fusion.14
  100.4 72.7 %all-gather.3.cloned.1.call-done = bf16[1,512,4096]{2,1,0:T(8,128)(2,1)} async-done(((bf16[1,128,4096]{2,1,0:T(8,128)(2,1)}), bf16[1,512,4096]{2,1,0:T(8,128)(2,1)}) %all-gather.3.cloned.1.call-update) | async-done | bytes 4194320 | tf_op jit(solution)/shard_map/all_gather | solution.py:64
  173.1 18.0 %fusion.18 = bf16[1,4096,1024]{1,2,0:T(8,128)(2,1)} fusion(bf16[1,4096,1024]{1,2,0:T(8,128)(2,1)} %copy.76, bf16[1,512,4096]{2,1,0:T(8,128)(2,1)} %all-gather.5.cloned.1.call-done, f32[512,1024]{1,0:T(8,128)S(1)} %fusion.14, bf16[1,4096,1024]{2,1,0:T(8,128)(2,1)} %param.12, bf16[1,512,4096]{2,1,0:T(8,128)(2,1)} %all-gather.3.cloned.1.call-done), kind=kOutput, calls=%fused_computation.21 | convolution fusion | flops 8612478976 | bytes 35651584 | tf_op jit(solution)/shard_map/dot_general | solution.py:84
  191.1 11.1 fusion.19
  202.1 10.5 pad_maximum_fusion.1
  212.6 41.6 %copy.78 = bf16[2,4096,1024]{2,0,1:T(2,128)(2,1)} copy(bf16[2,4096,1024]{1,2,0:T(8,128)(2,1)} %pad_maximum_fusion.1) | data formatting | bytes 33554432 | tf_op jit(solution)/shard_map/stack | solution.py:93
  254.2 4.2 all-to-all-start
  258.4 8.9 copy.72
  267.3 10.4 copy.74
  277.7 8.9 copy.73
  286.6 10.4 copy.75
  297.0 8.9 copy.81
  305.8 10.4 copy.83
  316.2 8.9 copy.82
  325.1 10.3 copy.84
  335.5 280.1 %all-to-all-done = bf16[2,4096,1024]{2,0,1:T(2,128)(2,1)} async-done(((bf16[2,4096,1024]{2,0,1:T(2,128)(2,1)}), bf16[2,4096,1024]{2,0,1:T(2,128)(2,1)}, u32[]{:S(2)}, u32[]{:S(2)}) %all-to-all-start) | async-done | bytes 16777248 | tf_op jit(solution)/shard_map/all_to_all | solution.py:16
  615.6 16.4 %copy.79 = bf16[2,4096,1024]{2,1,0:T(8,128)(2,1)} copy(bf16[2,4096,1024]{2,0,1:T(2,128)(2,1)} %all-to-all-done) | data formatting | bytes 33554432 | tf_op jit(solution)/shard_map/all_to_all | solution.py:16
  632.0 40.2 %convert_bitcast_fusion = bf16[2,128,8,4,1024]{4,2,3,1,0:T(8,128)(2,1)} fusion(f32[1,4,128,4,1024]{4,1,3,2,0:T(4,128)} %copy.84, f32[1,4,128,4,1024]{4,1,3,2,0:T(4,128)} %copy.83, bf16[2,128,8,4,1024]{4,1,3,2,0:T(8,128)(2,1)} %bitcast.243, f32[1,4,128,4,1024]{4,1,3,2,0:T(4,128)} %copy.75, f32[1,4,128,4,1024]{4,1,3,2,0:T(4,128)} %copy.74, ...), kind=kOutput, calls=%fused_computation.15 | convolution fusion | flops 188743808 | bytes 67108960 | tf_op jit(solution)/shard_map/lmrkc,lpm->lrpkc/dot_general | solution.py:36
  672.2 22.9 %copy.85 = bf16[2,128,8,4,1024]{1,4,3,2,0:T(8,128)(2,1)} copy(bf16[2,128,8,4,1024]{4,2,3,1,0:T(8,128)(2,1)} %convert_bitcast_fusion) | data formatting | bytes 33554432 | tf_op jit(solution)/shard_map/convert_element_type | solution.py:38
  695.1 1.2 fusion.69
  696.3 1.3 fusion.68
  697.7 1.5 fusion.67
  699.2 1.5 fusion.66
  700.7 1.1 fusion.65
  701.8 1.1 fusion.64
  715.4 381.4 %all_to_all.20 = bf16[32,2,128,1024]{2,3,1,0:T(8,128)(2,1)S(1)} all-to-all(bf16[32,2,128,1024]{2,3,1,0:T(8,128)(2,1)S(1)} %fusion.38), channel_id=1, replica_groups=mesh['path'=8,'mod'=4] {'path','mod'}, dimensions={0} | all-to-all | bytes 33554432 | tf_op jit(solution)/shard_map/all_to_all | solution.py:41
  1096.8 6.3 fusion.83
  1103.1 11.9 %copy.86 = bf16[1,32,128,1024]{3,2,1,0:T(8,128)(2,1)} copy(bf16[1,32,128,1024]{2,3,0,1:T(8,128)(2,1)} %get-tuple-element.3) | data formatting | bytes 16777216 | tf_op jit(solution)/shard_map/slice | solution.py:101
  1115.0 11.9 %copy.87 = bf16[1,32,128,1024]{3,2,1,0:T(8,128)(2,1)} copy(bf16[1,32,128,1024]{2,3,0,1:T(8,128)(2,1)} %get-tuple-element.2) | data formatting | bytes 16777216 | tf_op jit(solution)/shard_map/slice | solution.py:102
  (37 shorter events, 13.8 us)
Async XLA Ops:
  7.2 85.1 %all-gather.5.cloned.1.call-start = ((), (), s32[]{:S(2)}) async-start(), calls=%async_computation.3 | async-start | bytes 5242880 | tf_op jit(solution)/shard_map/all_gather | solution.py:63
  7.9 165.2 %all-gather.3.cloned.1.call-start = ((), (), s32[]{:S(2)}) async-start(), calls=%async_computation.2 | async-start | bytes 5242880 | tf_op jit(solution)/shard_map/all_gather | solution.py:64
  191.1 11.1 copy-start.1
  254.2 361.4 %all-to-all-start = ((bf16[2,4096,1024]{2,0,1:T(2,128)(2,1)}), bf16[2,4096,1024]{2,0,1:T(2,128)(2,1)}, u32[]{:S(2)}, u32[]{:S(2)}) async-start(bf16[2,4096,1024]{2,0,1:T(2,128)(2,1)} %copy.78), calls=%async_computation | async-start | bytes 33554432 | tf_op jit(solution)/shard_map/all_to_all | solution.py:16
  316.2 19.2 %copy-start.2 = (s32[8,2]{0,1:T(2,128)S(1)}, s32[8,2]{0,1:T(2,128)}, u32[]{:S(2)}) copy-start(s32[8,2]{0,1:T(2,128)} %param.17) | copy-start | bytes 196
  695.1 19.0 %copy-start = (bf16[2,128,8,4,1024]{1,4,3,2,0:T(8,128)(2,1)S(1)}, bf16[2,128,8,4,1024]{1,4,3,2,0:T(8,128)(2,1)}, u32[]{:S(2)}) copy-start(bf16[2,128,8,4,1024]{1,4,3,2,0:T(8,128)(2,1)} %copy.85) | copy-start | bytes 50331652
Sparse Core Ops, SparseCore 0:
  9.5 82.6 all-gather.4
  93.8 79.2 all-gather.2
